TPU v7x, 32 devices: a whole 2x2x4 slice. The times are simulated.
32 devices in a mesh: dp: 2 (over y), expert: 16 (over z, x, core).
Axes of the slice: x: 2, y: 2, z: 4, core: 2. Of those that a mesh axis runs over, the one named last changes fastest.
Arguments:
- routed: bfloat16 [4096, 7168], P(('dp', 'expert')), may hold values from -160 to 160
- expert_ids: int32 [4096, 8], P(('dp', 'expert')), may hold values from 0 to 127, all different within a row
- norm_gain: bfloat16 [7168], replicated, may hold values from 0.099609375 to 1.8984375
- gate_weight: bfloat16 [16, 7168, 2048], P('expert', None, 'dp'), may hold values from -0.0625 to 0.0625
- up_weight: bfloat16 [16, 7168, 2048], P('expert', None, 'dp'), may hold values from -0.0625 to 0.0625
- down_weight: bfloat16 [16, 2048, 7168], P('expert', 'dp'), may hold values from -0.125 to 0.125
- old_place: int32 [16], replicated, may hold values from 0 to 127, as said below
- new_place: int32 [16], replicated, may hold values from 0 to 127, as said below
- probe_ids: int32 [1280], P(('dp', 'expert')), may hold values from 0 to 127
Outputs:
- expert_load: float32 [128], P('expert')
- expert_energy: float32 [128], P('expert')
- probe_out: bfloat16 [1280, 7168], P(('dp', 'expert'))
Inputs may be any that keep to these rules, and one draw needn't show every extreme that they name: `old_place`: 16 different experts. `new_place`: the same 16 experts as old_place, in some order.
All inputs are finite; a program needn't handle non-finite values.
Results may differ from a plain program's by a relative error of at most 0.012.
Values may be sent and summed in bfloat16 or wider, within the bound.
A program may use at most 128 MiB of HBM per device.

v0:
```python
import functools

import jax
import jax.numpy as jnp
from jax import lax
from jax.experimental import pallas as pl
from jax.experimental.pallas import tpu as pltpu
from jax.sharding import PartitionSpec as P

EXP_DEV = 8
LANES = 128
MESH = pl.DeviceIdType.MESH
VMEM = pl.BlockSpec(memory_space=pltpu.VMEM)
SMEM = pl.BlockSpec(memory_space=pltpu.SMEM)
epsilon = 1e-06


def piece_width(width, n):
    w = LANES * -(-width // (LANES * n))
    while width % w:
        w += LANES
    return w


def prepare_kernel(routed, ids, probe, gain, normed, stats):
    tokens, width = routed.shape
    experts = stats.shape[1]
    total = jnp.zeros((tokens, LANES), jnp.float32)
    for c in range(width // LANES):
        x = routed[:, c * LANES : (c + 1) * LANES].astype(jnp.float32)
        total = total + x * x
    mean_square = jnp.sum(total, axis=1, keepdims=True) / width
    lane = lax.broadcasted_iota(jnp.int32, (tokens, experts), 1)
    chosen = jnp.zeros((tokens, experts), jnp.float32)
    for k in range(ids.shape[1]):
        chosen = chosen + jnp.where(ids[:, k : k + 1] == lane, 1.0, 0.0)
    stats[...] = jnp.zeros_like(stats)
    stats[0:1, :] = jnp.sum(chosen, axis=0, keepdims=True)
    stats[1:2, :] = jnp.sum(chosen * mean_square, axis=0, keepdims=True)
    probes = probe.shape[0]
    row = lax.broadcasted_iota(jnp.int32, (tokens, tokens), 0)
    column = lax.broadcasted_iota(jnp.int32, (tokens, tokens), 1)
    flat = jnp.sum(jnp.where(row == column, mean_square, 0.0), axis=0, keepdims=True)
    pick = probe[...] == lax.broadcasted_iota(jnp.int32, (probes, tokens), 1)
    scale = lax.rsqrt(jnp.sum(jnp.where(pick, flat, 0.0), axis=1, keepdims=True) + epsilon)
    pick = jnp.where(pick, 1.0, 0.0).astype(jnp.bfloat16)
    step = 512 if width % 512 == 0 else LANES
    for c in range(width // step):
        cols = slice(c * step, (c + 1) * step)
        rows = jnp.dot(pick, routed[:, cols], preferred_element_type=jnp.float32)
        normed[:, cols] = (rows * scale * gain[:, cols].astype(jnp.float32)).astype(jnp.bfloat16)


def prepare(routed, expert_ids, probe_ids, norm_gain, experts):
    probes = probe_ids.shape[0]
    width = routed.shape[1]
    return pl.pallas_call(
        prepare_kernel,
        out_shape=(
            jax.ShapeDtypeStruct((probes, width), jnp.bfloat16),
            jax.ShapeDtypeStruct((8, experts), jnp.float32),
        ),
        in_specs=[VMEM] * 4,
        out_specs=(VMEM, VMEM),
        compiler_params=pltpu.CompilerParams(vmem_limit_bytes=16 << 20),
        cost_estimate=pl.CostEstimate(flops=10**8, bytes_accessed=3 << 20, transcendentals=0),
    )(routed, expert_ids, probe_ids.reshape(probes, 1), norm_gain.reshape(1, width))


def remote(src, dst, send, recv, device):
    return pltpu.make_async_remote_copy(
        src_ref=src, dst_ref=dst, send_sem=send, recv_sem=recv, device_id=device, device_id_type=MESH
    )


def greet(g, me, d, n):
    barrier = pltpu.get_barrier_semaphore()
    for k in range(1, n):
        pl.semaphore_signal(barrier, inc=1, device_id=(g, lax.rem(me + k, n)), device_id_type=MESH)
    for c in range(1, d):
        pl.semaphore_signal(barrier, inc=1, device_id=(lax.rem(g + c, d), me), device_id_type=MESH)
    pl.semaphore_wait(barrier, n - 1 + d - 1)


class Pieces:
    def __init__(self, width, n):
        self.n = n
        self.w = piece_width(width, n)
        self.count = width // self.w

    def of(self, i):
        p = (i * self.count + self.n - 1) // self.n
        return jnp.minimum(p, self.count - 1), (p < self.count) & ((p * self.n) // self.count == i)

    def cols(self, p):
        return pl.ds(pl.multiple_of(p * self.w, self.w), self.w)


def fused_kernel(d, n, lag, source, home, normed, stats, gate_hbm, up_hbm, down_hbm, out, totals,
                 wg, wu, wd, x, gate_sum, up_sum, hidden, partial, arrived, summed, relay, outbox, relay2, outbox2,
                 st_in, st_mid, st_dp, sw, sd, s1, r1, s2, r2, sy, ry, ss, rs, ssy, rsy, s3, r3, s4, r4, sz, rz):
    g, me = lax.axis_index("dp"), lax.axis_index("expert")
    rows, width = normed.shape
    pieces = Pieces(width, n)
    mine, relays = pieces.of(me)
    count = pieces.count
    tall = d * rows
    down_step = wd.shape[0] // sd.shape[0]

    loads = []
    for p in range(count):
        part = pl.ds(p * pieces.w, pieces.w)
        loads.append(pltpu.make_async_copy(gate_hbm.at[part, :], wg.at[part, :], sw.at[0, p]))
        loads.append(pltpu.make_async_copy(up_hbm.at[part, :], wu.at[part, :], sw.at[1, p]))
    for p in range(sd.shape[0]):
        part = pl.ds(p * down_step, down_step)
        loads.append(pltpu.make_async_copy(down_hbm.at[part, :], wd.at[part, :], sd.at[p]))
    for load in loads:
        load.start()
    greet(g, me, d, n)

    def first(k):
        t = lax.rem(me + k, n)
        p, ok = pieces.of(t)
        return remote(normed.at[:, pieces.cols(p)], relay.at[me], s1.at[k], r1.at[me], (g, t)), ok

    def first_in(k):
        s = lax.rem(me + n - k, n)
        return remote(normed.at[:, pieces.cols(mine)], relay.at[s], s1.at[k], r1.at[s], (g, s))

    def stat(k):
        t = lax.rem(me + k, n)
        return remote(stats, st_in.at[me], ss.at[k], rs.at[me], (g, t))

    def stat_in(k):
        s = lax.rem(me + n - k, n)
        return remote(stats, st_in.at[s], ss.at[k], rs.at[s], (g, s))

    def second(k):
        j = lax.rem(me + k, n)
        return remote(outbox.at[j], x.at[g, :, pieces.cols(mine)], s2.at[k], r2.at[mine], (g, j))

    def along(p, c):
        here = x.at[g, :, pieces.cols(p)]
        return remote(here, here, sy.at[c, p], ry.at[g, p], (lax.rem(g + c, d), me))

    for k in range(1, n):
        copy, ok = first(k)
        pl.when(ok)(copy.start)
    for k in range(1, n):
        stat(k).start()
    st_in[me] = stats[...]
    gate_sum[...] = jnp.zeros_like(gate_sum)
    up_sum[...] = jnp.zeros_like(up_sum)

    @pl.when(relays)
    def _():
        relay[me] = normed[:, pieces.cols(mine)]
        for k in range(1, n):
            first_in(k).wait_recv()
        for k in range(1, n):
            j = lax.rem(me + k, n)
            outbox[j] = relay[source[j]]
            second(k).start()
        x[g, :, pieces.cols(mine)] = relay[source[me]]

    for load in loads:
        load.wait()

    def take(k):
        i = lax.rem(me + n - k, n)
        p, ok = pieces.of(i)

        @pl.when(ok)
        def _():
            @pl.when(k > 0)
            def _():
                remote(outbox.at[i], x.at[g, :, pieces.cols(p)], s2.at[k], r2.at[p], (g, i)).wait_recv()
            for c in range(1, d):
                along(p, c).start()

    def absorb(k):
        p, ok = pieces.of(lax.rem(me + n - k, n))

        @pl.when(ok)
        def _():
            for c in range(1, d):
                f = lax.rem(g + d - c, d)
                there = x.at[f, :, pieces.cols(p)]
                remote(there, there, sy.at[c, p], ry.at[f, p], (f, me)).wait_recv()
            part = x[:, :, pieces.cols(p)].astype(jnp.float32).reshape(tall, pieces.w).astype(jnp.bfloat16)
            gate_sum[...] += jnp.dot(part, wg[pieces.cols(p), :], preferred_element_type=jnp.float32)
            up_sum[...] += jnp.dot(part, wu[pieces.cols(p), :], preferred_element_type=jnp.float32)

    for k in range(lag):
        take(k)

    @pl.loop(lag, n)
    def _(k):
        take(k)
        absorb(k - lag)

    @pl.loop(n - lag, n)
    def _(k):
        absorb(k)

    gate = gate_sum[...]
    hidden[...] = (gate / (1.0 + jnp.exp(-gate)) * up_sum[...]).astype(jnp.bfloat16)

    def home_copy(p, c):
        t = lax.rem(g + c, d)
        return remote(partial.at[p, t], arrived.at[g, p], sz.at[c, p], rz.at[g, p], (t, me))

    def third(p, k, t):
        return remote(summed.at[p], relay2.at[me], s3.at[k], r3.at[me], (g, t))

    def fourth(k):
        j = lax.rem(me + k, n)
        return remote(outbox2.at[j], out.at[:, pieces.cols(mine)], s4.at[k], r4.at[mine], (g, j))

    def make(k):
        p, ok = pieces.of(lax.rem(me + k, n))

        @pl.when(ok)
        def _():
            value = jnp.dot(hidden[...], wd[:, pieces.cols(p)], preferred_element_type=jnp.float32)
            partial[p] = value.reshape(d, rows, pieces.w).astype(jnp.bfloat16)
            for c in range(1, d):
                home_copy(p, c).start()

    def add(k):
        t = lax.rem(me + k, n)
        p, ok = pieces.of(t)

        @pl.when(ok)
        def _():
            for c in range(1, d):
                f = lax.rem(g + d - c, d)
                remote(partial.at[p, f], arrived.at[f, p], sz.at[c, p], rz.at[f, p], (f, me)).wait_recv()
            arrived[g, p] = partial[p, g]
            total = arrived[0, p].astype(jnp.float32)
            for f in range(1, d):
                total = total + arrived[f, p].astype(jnp.float32)

            @pl.when(t != me)
            def _():
                summed[p] = total.astype(jnp.bfloat16)
                third(p, k, t).start()

            @pl.when(t == me)
            def _():
                relay2[me] = total.astype(jnp.bfloat16)

    @pl.loop(1, lag + 1)
    def _(k):
        make(k)

    @pl.loop(lag + 1, n + 1)
    def _(k):
        make(k)
        add(k - lag)

    @pl.loop(n + 1 - lag, n + 1)
    def _(k):
        add(k)

    for k in range(1, n):
        stat_in(k).wait_recv()
    mid = st_in[0]
    for s in range(1, n):
        mid = mid + st_in[s]
    st_mid[...] = mid
    st_dp[g] = mid
    for c in range(1, d):
        remote(st_mid, st_dp.at[g], ssy.at[c], rsy.at[g], (lax.rem(g + c, d), me)).start()

    @pl.when(relays)
    def _():
        for k in range(1, n):
            s = lax.rem(me + n - k, n)
            remote(summed.at[mine], relay2.at[s], s3.at[k], r3.at[s], (g, s)).wait_recv()
        for k in range(1, n):
            j = lax.rem(me + k, n)
            outbox2[j] = relay2[home[j]]
            fourth(k).start()
        out[:, pieces.cols(mine)] = relay2[home[me]]

    for c in range(1, d):
        f = lax.rem(g + d - c, d)
        remote(st_mid, st_dp.at[f], ssy.at[c], rsy.at[f], (f, me)).wait_recv()
    total = st_dp[0]
    for f in range(1, d):
        total = total + st_dp[f]
    totals[...] = total

    for k in range(1, n):
        copy, ok = first(k)
        pl.when(ok)(copy.wait_send)
        stat(k).wait_send()
    for c in range(1, d):
        remote(st_mid, st_dp.at[g], ssy.at[c], rsy.at[g], (lax.rem(g + c, d), me)).wait_send()
        for p in range(count):
            along(p, c).wait_send()
            home_copy(p, c).wait_send()
    for k in range(1, n):
        t = lax.rem(me + k, n)
        p, ok = pieces.of(t)
        pl.when(ok)(third(p, k, t).wait_send)

    @pl.when(relays)
    def _():
        for k in range(1, n):
            second(k).wait_send()
            fourth(k).wait_send()

    for k in range(1, n):
        i = lax.rem(me + n - k, n)
        p, ok = pieces.of(i)

        @pl.when(ok)
        def _():
            remote(outbox2.at[i], out.at[:, pieces.cols(p)], s4.at[k], r4.at[p], (g, i)).wait_recv()


def fused(normed, stats, source, home, gate, up, down, d, n):
    rows, width = normed.shape
    pieces = Pieces(width, n)
    units = gate.shape[1]
    count, w = pieces.count, pieces.w
    dma = pltpu.SemaphoreType.DMA
    block = lambda *shape: pltpu.VMEM(shape, jnp.bfloat16)
    wide = lambda *shape: pltpu.VMEM(shape, jnp.float32)
    anywhere = pl.BlockSpec(memory_space=pltpu.HBM)
    return pl.pallas_call(
        functools.partial(fused_kernel, d, n, 4),
        out_shape=(
            jax.ShapeDtypeStruct((rows, width), jnp.bfloat16),
            jax.ShapeDtypeStruct(stats.shape, jnp.float32),
        ),
        in_specs=[SMEM, SMEM, VMEM, VMEM, anywhere, anywhere, anywhere],
        out_specs=(VMEM, VMEM),
        scratch_shapes=[
            block(width, units), block(width, units), block(units, width),
            block(d, rows, width),
            wide(d * rows, units), wide(d * rows, units), block(d * rows, units),
            block(count, d, rows, w), block(d, count, rows, w), block(count, rows, w),
            block(n, rows, w), block(n, rows, w), block(n, rows, w), block(n, rows, w),
            wide(n, *stats.shape), wide(*stats.shape), wide(d, *stats.shape),
            dma((2, count)), dma((8,)),
            dma((n,)), dma((n,)), dma((n,)), dma((count,)), dma((d, count)), dma((d, count)),
            dma((n,)), dma((n,)), dma((d,)), dma((d,)),
            dma((n,)), dma((n,)), dma((n,)), dma((count,)), dma((d, count)), dma((d, count)),
        ],
        compiler_params=pltpu.CompilerParams(
            collective_id=0, has_side_effects=True, vmem_limit_bytes=62 << 20
        ),
    )(source, home, normed, stats, gate, up, down)


def on_device(
    routed,
    expert_ids,
    norm_gain,
    gate_weight,
    up_weight,
    down_weight,
    old_place,
    new_place,
    probe_ids,
):
    n, d = lax.axis_size("expert"), lax.axis_size("dp")
    experts = EXP_DEV * n
    tokens = routed.shape[0] * d * n
    normed, stats = prepare(routed, expert_ids, probe_ids, norm_gain, experts)
    slot_index = jnp.arange(n, dtype=jnp.int32)
    matches = new_place[:, None] == old_place[None, :]
    sources = jnp.sum(jnp.where(matches, slot_index[None, :], 0), axis=1)
    targets = jnp.sum(jnp.where(matches, slot_index[:, None], 0), axis=0)
    probe_out, totals = fused(
        normed, stats, targets, sources, gate_weight[0], up_weight[0], down_weight[0], d, n
    )
    owned = lax.dynamic_slice_in_dim(totals, lax.axis_index("expert") * EXP_DEV, EXP_DEV, 1)
    expert_load = owned[0] * experts / (tokens * expert_ids.shape[1])
    expert_energy = owned[1] / owned[0]
    return (expert_load, expert_energy, probe_out)


def solution(mesh):
    in_specs = (
        P(("dp", "expert"), None),
        P(("dp", "expert"), None),
        P(),
        P("expert", None, "dp"),
        P("expert", None, "dp"),
        P("expert", "dp", None),
        P(),
        P(),
        P(("dp", "expert")),
    )
    out_specs = (P("expert"), P("expert"), P(("dp", "expert"), None))
    return jax.shard_map(
        on_device, mesh=mesh, in_specs=in_specs, out_specs=out_specs, check_vma=False
    )
```

profile of v0, /device:TPU:27, one launch (start us, length us, event | category | flops | bytes accessed | tf_op | source)
XLA Modules:
  0.0 91.7 jit_solution(3017130459741557474)
XLA Ops:
  0.6 1.4 %fusion.1 = (s32[16]{0:T(128)}, s32[16]{0:T(128)}) fusion(s32[16]{0:T(128)} %param.15, s32[16]{0:T(128)} %param.16), kind=kLoop, calls=%fused_computation.3 | loop fusion | flops 1248 | bytes 256 | tf_op jit(solution)/shard_map/reduce_sum | solution.py:377
  2.0 0.8 copy.14.ids
  2.8 0.7 copy.15.probe
  3.5 0.7 reshape.18.gain
  4.3 0.0 copy-start
  4.3 1.5 %copy-done = bf16[128,7168]{1,0:T(8,128)(2,1)S(1)} copy-done((bf16[128,7168]{1,0:T(8,128)(2,1)S(1)}, bf16[128,7168]{1,0:T(8,128)(2,1)}, u32[]{:S(2)}) %copy-start) | copy-done | bytes 1835032
  5.8 0.7 shard_map.112
  6.5 0.0 copy-start.1
  6.5 0.8 copy-done.1
  7.3 0.0 copy-start.2
  7.3 0.6 copy-done.2
  7.9 80.6 %shard_map.113 = (bf16[40,7168]{1,0:T(8,128)(2,1)}, f32[8,128]{1,0:T(8,128)}) custom-call(s32[16]{0:T(128)} %get-tuple-element.12.source, s32[16]{0:T(128)} %get-tuple-element.11.home, bf16[40,7168]{1,0:T(8,128)(2,1)} %copy-done.1, f32[8,128]{1,0:T(8,128)} %copy-done.2, bf16[7168,1024]{1,0:T(8,128)(2,1)} %bitcast.8, bf16[7168,1024]{1,0:T(8,128)(2,1)} %bitcast.9, ...), custom_call_target="tpu_custom_call" | custom-call | tf_op jit(solution)/shard_map/pallas_call | solution.py:334
  88.6 0.7 constant_dynamic-slice_fusion
  89.3 0.5 fusion.2
  89.8 1.9 %copy.17 = bf16[40,7168]{1,0:T(8,128)(2,1)} copy(bf16[40,7168]{1,0:T(8,128)(2,1)} %get-tuple-element.20) | data formatting | bytes 1146880
Async XLA Ops:
  4.3 1.5 %copy-start = (bf16[128,7168]{1,0:T(8,128)(2,1)S(1)}, bf16[128,7168]{1,0:T(8,128)(2,1)}, u32[]{:S(2)}) copy-start(bf16[128,7168]{1,0:T(8,128)(2,1)} %routed.1) | copy-start | bytes 5505028
  6.5 0.8 copy-start.1
  7.3 0.6 copy-start.2
where the time goes:
time: 92.1 us; the launch traced here: 91.7 us
  Pallas kernels  81.4 us (88%)
  local copies, waits for them, and re-layouts  7.79 us (8%)
  other arithmetic  1.9 us (2%)
    pallas_call x1, Pallas kernels, fused(): pl.pallas_call(functools.partial(fused_kernel, d, n, 4), out_shape=(jax.S...  80.6 us
    unnamed x8, local copies, waits for them, and re-layouts  5.58 us

commit v1 on v0

v1 whole, which is shorter than its diff:
```python
import functools

import jax
import jax.numpy as jnp
from jax import lax
from jax.experimental import pallas as pl
from jax.experimental.pallas import tpu as pltpu
from jax.sharding import PartitionSpec as P

EXP_DEV = 8
LANES = 128
MESH = pl.DeviceIdType.MESH
VMEM = pl.BlockSpec(memory_space=pltpu.VMEM)
SMEM = pl.BlockSpec(memory_space=pltpu.SMEM)
HBM = pl.BlockSpec(memory_space=pltpu.HBM)
epsilon = 1e-06
PAIR = 2
MOST = 8
LAGS = (1, 3, 5, 7, 2, 3, 4, 6)


def chunking(width, relays):
    units = width // (relays * LANES)
    assert units * relays * LANES == width
    count = max(c for c in range(1, MOST + 1) if units % c == 0)
    return count, units // count * LANES


def remote(src, dst, send, recv, device):
    return pltpu.make_async_remote_copy(
        src_ref=src, dst_ref=dst, send_sem=send, recv_sem=recv, device_id=device, device_id_type=MESH
    )


def greet(g, me, d, n):
    barrier = pltpu.get_barrier_semaphore()
    for k in range(1, n):
        pl.semaphore_signal(barrier, inc=1, device_id=(g, lax.rem(me + k, n)), device_id_type=MESH)
    for c in range(1, d):
        pl.semaphore_signal(barrier, inc=1, device_id=(lax.rem(g + c, d), me), device_id_type=MESH)


def meet(d, n):
    pl.semaphore_wait(pltpu.get_barrier_semaphore(), n - 1 + d - 1)


def prepare(routed, probe, gain, normed):
    tokens, width = routed.shape
    probes = probe.shape[1]
    total = jnp.zeros((tokens, LANES), jnp.float32)
    for c in range(width // LANES):
        v = routed[:, c * LANES : (c + 1) * LANES].astype(jnp.float32)
        total = total + v * v
    mean_square = jnp.sum(total, axis=1, keepdims=True) / width
    row = lax.broadcasted_iota(jnp.int32, (tokens, tokens), 0)
    column = lax.broadcasted_iota(jnp.int32, (tokens, tokens), 1)
    flat = jnp.sum(jnp.where(row == column, mean_square, 0.0), axis=0, keepdims=True)
    pick = jnp.where(probe[...] == lax.broadcasted_iota(jnp.int32, (tokens, probes), 0), 1.0, 0.0).T
    scale = lax.rsqrt(jnp.sum(pick * flat, axis=1, keepdims=True) + epsilon)
    pick = pick.astype(jnp.bfloat16)
    step = 512 if width % 512 == 0 else LANES
    for c in range(width // step):
        cols = slice(c * step, (c + 1) * step)
        rows = jnp.dot(pick, routed[:, cols], preferred_element_type=jnp.float32)
        normed[:, cols] = (rows * scale * gain[:, cols].astype(jnp.float32)).astype(jnp.bfloat16)
    return mean_square


def statistics(ids, mean_square, stats):
    tokens, experts = mean_square.shape[0], stats.shape[1]
    lane = lax.broadcasted_iota(jnp.int32, (tokens, experts), 1)
    by_token = ids[...].T
    chosen = jnp.zeros((tokens, experts), jnp.float32)
    for k in range(by_token.shape[1]):
        chosen = chosen + jnp.where(by_token[:, k : k + 1] == lane, 1.0, 0.0)
    stats[0:1, :] = jnp.sum(chosen, axis=0, keepdims=True)
    stats[1:2, :] = jnp.sum(chosen * mean_square, axis=0, keepdims=True)


def inverse(wanted, held, result, n):
    @pl.loop(0, n)
    def _(j):
        value = jnp.int32(0)
        for s in range(n):
            value = value + jnp.where(wanted[j] == held[s], s, 0)
        result[j] = value


def plan(sources, h, half, crossing, pick, cross):
    own, other = h * half, (1 - h) * half
    rank = jnp.int32(0)
    for j in range(half):
        local = sources[own + j] - own
        away = (local < 0) | (local >= half)
        pick[j] = jnp.where(away, half + jnp.minimum(rank, crossing - 1), local)
        rank = rank + jnp.where(away, 1, 0)
    rank = jnp.int32(0)
    found = [jnp.int32(0)] * crossing
    for j in range(half):
        local = sources[other + j] - own
        here = (local >= 0) & (local < half)
        for i in range(min(j + 1, crossing)):
            found[i] = jnp.where(here & (rank == i), local, found[i])
        rank = rank + jnp.where(here, 1, 0)
    for i in range(crossing):
        cross[i] = found[i]


def selection(matrix, table, rows):
    shape = (rows, matrix.shape[1])
    row = lax.broadcasted_iota(jnp.int32, shape, 0)
    column = lax.broadcasted_iota(jnp.int32, shape, 1)
    for j in range(table.shape[0]):
        chosen = column == table[j] * rows + row
        matrix[j * rows : (j + 1) * rows, :] = jnp.where(chosen, 1.0, 0.0).astype(jnp.bfloat16)


def select(matrix, blocks):
    slots, rows, width = blocks.shape
    flat = blocks.astype(jnp.float32).reshape(slots * rows, width).astype(jnp.bfloat16)
    value = jnp.dot(matrix[...], flat, preferred_element_type=jnp.float32)
    return value.reshape(matrix.shape[0] // rows, rows, width).astype(jnp.bfloat16)


def pipeline(count, stages):
    @pl.loop(0, count + max(lag for _, lag in stages))
    def _(t):
        for stage, lag in stages:
            @pl.when((t >= lag) & (t < count + lag))
            def _():
                stage(t - lag)


class Layout:
    def __init__(self, g, me, n, width):
        self.half, self.relays = n // 2, n // 4
        self.count, self.w = chunking(width, self.relays)
        self.wide = self.relays * self.w
        self.pairs = max(1, self.relays // PAIR)
        self.group = self.relays // self.pairs
        self.g, self.me = g, me
        self.h, self.slot = me // self.half, lax.rem(me, self.half)
        self.base = self.h * self.half
        self.r = lax.rem(me, self.relays)
        self.is_relay = me // self.relays == 1 + self.h
        self.outer = self.base + self.h * self.relays
        self.outer_slot = self.h * self.relays
        self.first = (1 + self.h) * self.relays
        self.partner = me + self.relays - 2 * self.relays * self.h
        self.line, self.lane = self.r // self.group, lax.rem(self.r, self.group)

    def piece(self, c, rr, size=1):
        return pl.ds(pl.multiple_of(c * self.wide + rr * self.w, self.w), size * self.w)

    def chunk(self, c):
        return pl.ds(pl.multiple_of(c * self.wide, self.wide), self.wide)


class Route:
    def __init__(self, lay, crossing, take, put, load, store, pick, cross, bufs, sems):
        self.lay, self.crossing, self.take, self.put = lay, crossing, take, put
        self.load, self.store, self.pick, self.cross = load, store, pick, cross
        self.side, self.pool, self.over, self.deal = bufs
        self.ss, self.rs, self.sl, self.rl, self.sf, self.sx, self.rx, self.sg, self.rg = sems

    def direct(self, c, rr):
        l = self.lay
        return remote(
            self.take(c, rr, 1), self.pool.at[c, l.slot], self.ss.at[c, rr], self.rs.at[c, l.slot], (l.g, l.first + rr)
        )

    def direct_in(self, c, s):
        l = self.lay
        return remote(self.take(c, l.r, 1), self.pool.at[c, s], self.ss.at[c, l.r], self.rs.at[c, s], (l.g, l.base + s))

    def sideways(self, c, line):
        l = self.lay
        return remote(
            self.take(c, line * l.group, l.group), self.side.at[c, l.line], self.sl.at[c, line], self.rl.at[c, l.line],
            (l.g, l.outer + line * l.group + l.lane),
        )

    def sideways_in(self, c, line):
        l = self.lay
        return remote(
            self.take(c, line * l.group, l.group), self.side.at[c, line], self.sl.at[c, line], self.rl.at[c, line],
            (l.g, l.outer + line * l.group + l.lane),
        )

    def onward(self, c, line, q):
        l = self.lay
        rr = l.line * l.group + q
        s = l.outer_slot + line * l.group + l.lane
        return remote(
            self.side.at[c, line, :, pl.ds(q * l.w, l.w)], self.pool.at[c, s], self.sf.at[c, line, q],
            self.rs.at[c, s], (l.g, l.first + rr),
        )

    def across(self, c):
        l = self.lay
        return remote(
            self.over.at[c], self.pool.at[c, pl.ds(l.half, self.crossing)], self.sx.at[c], self.rx.at[c], (l.g, l.partner)
        )

    def give(self, c, j):
        l = self.lay
        return remote(self.deal.at[c, j], self.put(c, l.r), self.sg.at[c, j], self.rg.at[c, l.r], (l.g, l.base + j))

    def given(self, c, rr):
        l = self.lay
        return remote(self.deal.at[c, l.slot], self.put(c, rr), self.sg.at[c, l.slot], self.rg.at[c, rr], (l.g, l.first + rr))

    def others(self, stage):
        l = self.lay
        for rr in range(l.relays):
            pl.when(l.first + rr != l.me)(functools.partial(stage, rr))

    def lines(self, stage):
        l = self.lay
        for line in range(l.pairs):
            pl.when(jnp.logical_not(l.is_relay) & (line != l.line))(functools.partial(stage, line))

    def near(self, stage):
        l = self.lay
        for rr in range(l.relays):
            pl.when(jnp.where(l.is_relay, rr != l.r, rr // l.group == l.line))(functools.partial(stage, rr))

    def start_far(self, c):
        self.lines(lambda line: self.sideways(c, line).start())

    def start_near(self, c):
        self.near(lambda rr: self.direct(c, rr).start())

    def forward(self, c):
        l = self.lay

        def stage(line):
            self.sideways_in(c, line).wait_recv()
            for q in range(l.group):
                self.onward(c, line, q).start()

        self.lines(stage)

    def collect(self, c):
        l = self.lay

        @pl.when(l.is_relay)
        def _():
            self.pool[c, l.slot] = self.load(c, l.r)
            for k in range(1, l.half):
                self.direct_in(c, lax.rem(l.slot + k, l.half)).wait_recv()
            self.over[c] = select(self.cross, self.pool[c, : l.half])
            self.across(c).start()

    def hand(self, c):
        l = self.lay

        @pl.when(l.is_relay)
        def _():
            self.across(c).wait_recv()
            self.deal[c] = select(self.pick, self.pool[c])
            for k in range(1, l.half):
                self.give(c, lax.rem(l.slot + k, l.half)).start()
            self.store(c, l.r, self.deal[c, l.slot])

    def arrive(self, c):
        self.others(lambda rr: self.given(c, rr).wait_recv())

    def drain(self, c):
        l = self.lay
        self.near(lambda rr: self.direct(c, rr).wait_send())

        def stage(line):
            self.sideways(c, line).wait_send()
            for q in range(l.group):
                self.onward(c, line, q).wait_send()

        self.lines(stage)

        @pl.when(l.is_relay)
        def _():
            self.across(c).wait_send()
            for k in range(1, l.half):
                self.give(c, lax.rem(l.slot + k, l.half)).wait_send()


def fused_kernel(d, n, crossing, lags, old, new, routed_hbm, ids, probe, gain, gate_hbm, up_hbm, down_hbm, out, totals,
                 wg, wu, wd, routed, normed, x, gate_sum, up_sum, hidden, partial, arrived, summed,
                 stats, st_in, st_mid, st_dp, source, holder, order, crossed, pick, cross, pick2, cross2, sl, sw, sd,
                 sy, ry, ss, rs, ssy, rsy, sz, rz, *rest):
    g, me = lax.axis_index("dp"), lax.axis_index("expert")
    rows, width = normed.shape
    lay = Layout(g, me, n, width)
    count, wide, w = lay.count, lay.wide, lay.w
    chunk, piece = lay.chunk, lay.piece
    tall = d * rows
    down_step = wd.shape[0] // sd.shape[0]

    greet(g, me, d, n)
    load_routed = pltpu.make_async_copy(routed_hbm, routed, sl)
    load_routed.start()
    weights, downs = [], []
    for c in range(count):
        part = pl.ds(c * wide, wide)
        weights.append(pltpu.make_async_copy(gate_hbm.at[part, :], wg.at[part, :], sw.at[0, c]))
        weights.append(pltpu.make_async_copy(up_hbm.at[part, :], wu.at[part, :], sw.at[1, c]))
    for p in range(sd.shape[0]):
        part = pl.ds(p * down_step, down_step)
        downs.append(pltpu.make_async_copy(down_hbm.at[part, :], wd.at[part, :], sd.at[p]))
    inverse(old, new, source, n)
    inverse(new, old, holder, n)
    for places, picks, crosses in ((source, pick, cross), (holder, pick2, cross2)):
        plan(places, lay.h, lay.half, crossing, order, crossed)
        selection(picks, order, rows)
        selection(crosses, crossed, rows)
    load_routed.wait()
    for load in weights + downs:
        load.start()
    mean_square = prepare(routed, probe, gain, normed)
    meet(d, n)

    def put_x(c, rr, value):
        x[g, :, piece(c, rr)] = value

    def put_out(c, rr, value):
        out[:, piece(c, rr)] = value

    there = Route(
        lay, crossing,
        lambda c, rr, size: normed.at[:, piece(c, rr, size)], lambda c, rr: x.at[g, :, piece(c, rr)],
        lambda c, rr: normed[:, piece(c, rr)], put_x, pick, cross, rest[0:4], rest[8:17],
    )
    summed_piece = lambda rr, size: pl.ds(pl.multiple_of(rr * w, w), size * w)
    home = Route(
        lay, crossing,
        lambda c, rr, size: summed.at[c, :, summed_piece(rr, size)], lambda c, rr: out.at[:, piece(c, rr)],
        lambda c, rr: summed[c, :, summed_piece(rr, 1)], put_out, pick2, cross2, rest[4:8], rest[17:26],
    )

    def along(c, q):
        here = x.at[g, :, chunk(c)]
        return remote(here, here, sy.at[c, q], ry.at[c, g], (lax.rem(g + q, d), me))

    def along_in(c, q):
        f = lax.rem(g + d - q, d)
        other = x.at[f, :, chunk(c)]
        return remote(other, other, sy.at[c, q], ry.at[c, f], (f, me))

    def stat(k):
        return remote(stats, st_in.at[me], ss.at[k], rs.at[me], (g, lax.rem(me + k, n)))

    def stat_in(k):
        s = lax.rem(me + n - k, n)
        return remote(stats, st_in.at[s], ss.at[k], rs.at[s], (g, s))

    def stat_dp(q):
        return remote(st_mid, st_dp.at[g], ssy.at[q], rsy.at[g], (lax.rem(g + q, d), me))

    ahead = min(2, count)
    pl.loop(0, count)(there.start_far)
    pl.loop(0, ahead)(there.start_near)
    pl.when(lay.is_relay)(lambda: pl.loop(ahead, count)(there.start_near))

    statistics(ids, mean_square, stats)
    for k in range(1, n):
        stat(k).start()
    st_in[me] = stats[...]
    gate_sum[...] = jnp.zeros_like(gate_sum)
    up_sum[...] = jnp.zeros_like(up_sum)

    def forward(c):
        there.forward(c)
        pl.when(jnp.logical_not(lay.is_relay) & (c + ahead < count))(lambda: there.start_near(c + ahead))

    def take(c):
        there.arrive(c)
        for q in range(1, d):
            along(c, q).start()

    def absorb(c):
        for q in range(1, d):
            along_in(c, q).wait_recv()
        part = x[:, :, chunk(c)].astype(jnp.float32).reshape(tall, wide).astype(jnp.bfloat16)
        for k, (hbm, ref, total) in enumerate(((gate_hbm, wg, gate_sum), (up_hbm, wu, up_sum))):
            pltpu.make_async_copy(hbm.at[chunk(c), :], ref.at[chunk(c), :], sw.at[k, c]).wait()
            total[...] += jnp.dot(part, ref[chunk(c), :], preferred_element_type=jnp.float32)

    pipeline(count, [
        (forward, 0), (there.collect, lags[0]), (there.hand, lags[1]), (take, lags[2]), (absorb, lags[3]),
    ])

    gate = gate_sum[...]
    hidden[...] = (gate / (1.0 + jnp.exp(-gate)) * up_sum[...]).astype(jnp.bfloat16)
    for load in downs:
        load.wait()

    def home_copy(c, q):
        t = lax.rem(g + q, d)
        return remote(partial.at[c, t], arrived.at[c, g], sz.at[c, q], rz.at[c, g], (t, me))

    def home_in(c, q):
        f = lax.rem(g + d - q, d)
        return remote(partial.at[c, f], arrived.at[c, f], sz.at[c, q], rz.at[c, f], (f, me))

    def make(c):
        value = jnp.dot(hidden[...], wd[:, chunk(c)], preferred_element_type=jnp.float32)
        partial[c] = value.reshape(d, rows, wide).astype(jnp.bfloat16)
        for q in range(1, d):
            home_copy(c, q).start()

    def add(c):
        for q in range(1, d):
            home_in(c, q).wait_recv()
        total = partial[c, g].astype(jnp.float32)
        for q in range(1, d):
            total = total + arrived[c, lax.rem(g + q, d)].astype(jnp.float32)
        summed[c] = total.astype(jnp.bfloat16)
        home.start_far(c)
        home.start_near(c)

    for k in range(1, n):
        stat_in(k).wait_recv()
    mid = st_in[0]
    for s in range(1, n):
        mid = mid + st_in[s]
    st_mid[...] = mid
    st_dp[g] = mid
    for q in range(1, d):
        stat_dp(q).start()

    pipeline(count, [
        (make, 0), (add, lags[4]), (home.forward, lags[5]), (home.collect, lags[6]), (home.hand, lags[7]),
    ])

    for q in range(1, d):
        f = lax.rem(g + d - q, d)
        remote(st_mid, st_dp.at[f], ssy.at[q], rsy.at[f], (f, me)).wait_recv()
    total = st_dp[0]
    for f in range(1, d):
        total = total + st_dp[f]
    totals[...] = total

    for k in range(1, n):
        stat(k).wait_send()
    for q in range(1, d):
        stat_dp(q).wait_send()

    @pl.loop(0, count)
    def _(c):
        there.drain(c)
        home.drain(c)
        for q in range(1, d):
            along(c, q).wait_send()
            home_copy(c, q).wait_send()

    pl.loop(0, count)(home.arrive)


def fused(crossing, collective, d, n, experts, old, new, routed, ids, probe, gain, gate, up, down):
    tokens, width = routed.shape
    rows = probe.shape[1]
    units = gate.shape[1]
    lay = Layout(0, 0, n, width)
    count, w, half, relays, pairs, group = lay.count, lay.w, lay.half, lay.relays, lay.pairs, lay.group
    full = lay.wide
    dma = pltpu.SemaphoreType.DMA
    block = lambda *shape: pltpu.VMEM(shape, jnp.bfloat16)
    wide = lambda *shape: pltpu.VMEM(shape, jnp.float32)
    numbers = lambda size: pltpu.SMEM((size,), jnp.int32)
    matrices = [block(half * rows, (half + crossing) * rows), block(crossing * rows, half * rows)]
    bufs = [
        block(count, pairs, rows, group * w), block(count, half + crossing, rows, w),
        block(count, crossing, rows, w), block(count, half, rows, w),
    ]
    sems = [
        dma((count, relays)), dma((count, half)), dma((count, pairs)), dma((count, pairs)), dma((count, pairs, group)),
        dma((count,)), dma((count,)), dma((count, half)), dma((count, relays)),
    ]
    return pl.pallas_call(
        functools.partial(fused_kernel, d, n, crossing, LAGS),
        out_shape=(
            jax.ShapeDtypeStruct((rows, width), jnp.bfloat16),
            jax.ShapeDtypeStruct((2, experts), jnp.float32),
        ),
        in_specs=[SMEM, SMEM, HBM, VMEM, VMEM, VMEM, HBM, HBM, HBM],
        out_specs=(VMEM, VMEM),
        scratch_shapes=[
            block(width, units), block(width, units), block(units, width),
            block(tokens, width), block(rows, width), block(d, rows, width),
            wide(d * rows, units), wide(d * rows, units), block(d * rows, units),
            block(count, d, rows, full), block(count, d, rows, full), block(count, rows, full),
            wide(2, experts), wide(n, 2, experts), wide(2, experts), wide(d, 2, experts),
            numbers(n), numbers(n), numbers(half), numbers(crossing), *matrices, *matrices,
            dma, dma((2, count)), dma((8,)),
            dma((count, d)), dma((count, d)), dma((n,)), dma((n,)), dma((d,)), dma((d,)),
            dma((count, d)), dma((count, d)),
            *bufs, *bufs, *sems, *sems,
        ],
        compiler_params=pltpu.CompilerParams(
            collective_id=collective, has_side_effects=True, vmem_limit_bytes=62 << 20
        ),
    )(old, new, routed, ids, probe, gain, gate, up, down)


def on_device(
    routed,
    expert_ids,
    norm_gain,
    gate_weight,
    up_weight,
    down_weight,
    old_place,
    new_place,
    probe_ids,
):
    n, d = lax.axis_size("expert"), lax.axis_size("dp")
    experts = EXP_DEV * n
    tokens = routed.shape[0] * d * n
    half = n // 2
    widths = (half // 2, half * 5 // 8, half)
    index = jnp.arange(n, dtype=jnp.int32)
    apart = (index[:, None] < half) & (index[None, :] >= half)
    crossings = jnp.sum(((old_place[:, None] == new_place[None, :]) & apart).astype(jnp.int32))
    branch = (crossings > widths[0]).astype(jnp.int32) + (crossings > widths[1]).astype(jnp.int32)
    kernels = [functools.partial(fused, widths[i], i, d, n, experts) for i in range(3)]
    probe_out, totals = lax.switch(
        branch, kernels,
        old_place, new_place, routed, expert_ids.T, probe_ids.reshape(1, -1), norm_gain.reshape(1, -1),
        gate_weight[0], up_weight[0], down_weight[0],
    )
    owned = lax.dynamic_slice_in_dim(totals, lax.axis_index("expert") * EXP_DEV, EXP_DEV, 1)
    expert_load = owned[0] * experts / (tokens * expert_ids.shape[1])
    expert_energy = owned[1] / owned[0]
    return (expert_load, expert_energy, probe_out)


def solution(mesh):
    in_specs = (
        P(("dp", "expert"), None),
        P(("dp", "expert"), None),
        P(),
        P("expert", None, "dp"),
        P("expert", None, "dp"),
        P("expert", "dp", None),
        P(),
        P(),
        P(("dp", "expert")),
    )
    out_specs = (P("expert"), P("expert"), P(("dp", "expert"), None))
    return jax.shard_map(
        on_device, mesh=mesh, in_specs=in_specs, out_specs=out_specs, check_vma=False
    )
```

time: 92.1 us -> 79.1 us (0.86)
  the two profiles are of different devices: /device:TPU:27 before, /device:TPU:0 now
where the time goes in v1:
time: 79.1 us; the launch traced here: 78.8 us
  Pallas kernels  73.1 us (92%)
  between operations  1.96 us (2%)
  other arithmetic  1.91 us (2%)
  local copies, waits for them, and re-layouts  1.62 us (2%)
    pallas_call x1, Pallas kernels, fused(): pl.pallas_call(functools.partial(fused_kernel, d, n, crossing, LAGS), out...  73.1 us

profile of v1, /device:TPU:0, one launch (start us, length us, event | category | flops | bytes accessed | tf_op | source)
XLA Modules:
  0.0 78.8 jit_solution(288019089860201846)
XLA Ops:
  0.6 1.4 %convert_reduce_fusion = s32[]{:T(128)} fusion(s32[16]{0:T(128)} %param.19, s32[16]{0:T(128)} %param.18, pred[16]{0:T(512)(128)(4,1)S(1)} %get-tuple-element.90, pred[16]{0:T(512)(128)(4,1)S(1)} %get-tuple-element.91), kind=kLoop, calls=%fused_computation | loop fusion | flops 1279 | bytes 164 | tf_op jit(solution)/shard_map/reduce_sum | solution.py:523
  3.3 0.7 reshape.28
  4.1 73.3 %conditional.1 = ((bf16[40,7168]{1,0:T(8,128)(2,1)S(1)}, f32[2,128]{1,0:T(2,128)S(1)})) conditional(s32[]{:T(128)} %clamp.3, (s32[16]{0:T(128)}, s32[16]{0:T(128)}, bf16[128,7168]{1,0:T(8,128)(2,1)}, s32[8,128]{1,0:T(8,128)}, s32[1,40]{1,0:T(1,128)}, /*index=5*/bf16[1,7168]{1,0:T(2,128)(2,1)S(1)}, bf16[7168,1024]{1,0:T(8,128)(2,1)}, ...), branch_computations={%region_1.0_spmd, %region_2.0_spmd, %region_3.0_spmd} | conditional | bytes 8 | solution.py:526
  4.1 73.1 %branch_0_fun.1 = (bf16[40,7168]{1,0:T(8,128)(2,1)S(1)}, f32[2,128]{1,0:T(2,128)S(1)}) custom-call(s32[16]{0:T(128)} %get-tuple-element.54.old, s32[16]{0:T(128)} %get-tuple-element.55.new, bf16[128,7168]{1,0:T(8,128)(2,1)} %get-tuple-element.56.routed_hbm, s32[8,128]{1,0:T(8,128)} %get-tuple-element.57.ids, s32[1,40]{1,0:T(1,128)} %get-tuple-element.58.probe, ...), custom_call_target="tpu_custom_call" | custom-call | tf_op jit(solution)/shard_map/cond/branch_0_fun/pallas_call | solution.py:479
  77.4 0.1 constant_dynamic-slice_fusion
  77.4 0.5 fusion
  78.0 0.8 %copy.19 = bf16[40,7168]{1,0:T(8,128)(2,1)} copy(bf16[40,7168]{1,0:T(8,128)(2,1)S(1)} %get-tuple-element.103) | data formatting | bytes 1146880
  (1 shorter events, 0.0 us)

commit v2 on v1

--- a/solution.py
+++ b/solution.py
@@ -15,8 +15,10 @@
 HBM = pl.BlockSpec(memory_space=pltpu.HBM)
 epsilon = 1e-06
 PAIR = 2
-MOST = 8
-LAGS = (1, 3, 5, 7, 2, 3, 4, 6)
+AHEAD = 4
+EARLY = (3, 3)
+MOST = 14
+LAGS = {7: (2, 4, 6, 1, 2, 4, 6), 14: (4, 8, 12, 3, 5, 7, 10)}
 
 
 def chunking(width, relays):
@@ -157,89 +159,81 @@
 
 
 class Route:
-    def __init__(self, lay, crossing, take, put, load, store, pick, cross, bufs, sems):
+    def __init__(self, lay, crossing, early, take, put, load, store, pick, cross, bufs, sems):
         self.lay, self.crossing, self.take, self.put = lay, crossing, take, put
         self.load, self.store, self.pick, self.cross = load, store, pick, cross
         self.side, self.pool, self.over, self.deal = bufs
-        self.ss, self.rs, self.sl, self.rl, self.sf, self.sx, self.rx, self.sg, self.rg = sems
-
-    def direct(self, c, rr):
+        self.s_direct, self.s_early, self.s_side, self.s_onward, self.s_across, self.s_give = sems[:6]
+        self.r_direct, self.r_side, self.r_across, self.r_give = sems[6:]
+        self.early = early
+
+    def several(self, ref, send, recv):
+        return remote(ref, ref, send, recv, (self.lay.g, self.lay.partner))
+
+    def direct(self, c, rr, send):
+        l = self.lay
+        return remote(self.take(c, rr, 1), self.pool.at[c, l.slot], send, self.r_direct.at[c], (l.g, l.first + rr))
+
+    def sideways(self, c, line):
         l = self.lay
         return remote(
-            self.take(c, rr, 1), self.pool.at[c, l.slot], self.ss.at[c, rr], self.rs.at[c, l.slot], (l.g, l.first + rr)
-        )
-
-    def direct_in(self, c, s):
-        l = self.lay
-        return remote(self.take(c, l.r, 1), self.pool.at[c, s], self.ss.at[c, l.r], self.rs.at[c, s], (l.g, l.base + s))
-
-    def sideways(self, c, line):
-        l = self.lay
-        return remote(
-            self.take(c, line * l.group, l.group), self.side.at[c, l.line], self.sl.at[c, line], self.rl.at[c, l.line],
+            self.take(c, line * l.group, l.group), self.side.at[c, l.line], self.s_side, self.r_side.at[c],
             (l.g, l.outer + line * l.group + l.lane),
         )
 
-    def sideways_in(self, c, line):
+    def onward(self, c, line, q):
         l = self.lay
         return remote(
-            self.take(c, line * l.group, l.group), self.side.at[c, line], self.sl.at[c, line], self.rl.at[c, line],
-            (l.g, l.outer + line * l.group + l.lane),
+            self.side.at[c, line, :, pl.ds(q * l.w, l.w)], self.pool.at[c, l.outer_slot + line * l.group + l.lane],
+            self.s_onward, self.r_direct.at[c], (l.g, l.first + l.line * l.group + q),
         )
 
-    def onward(self, c, line, q):
-        l = self.lay
-        rr = l.line * l.group + q
-        s = l.outer_slot + line * l.group + l.lane
+    def across(self, c):
+        l = self.lay
         return remote(
-            self.side.at[c, line, :, pl.ds(q * l.w, l.w)], self.pool.at[c, s], self.sf.at[c, line, q],
-            self.rs.at[c, s], (l.g, l.first + rr),
+            self.over.at[c], self.pool.at[c, pl.ds(l.half, self.crossing)], self.s_across, self.r_across.at[c], (l.g, l.partner)
         )
 
-    def across(self, c):
-        l = self.lay
-        return remote(
-            self.over.at[c], self.pool.at[c, pl.ds(l.half, self.crossing)], self.sx.at[c], self.rx.at[c], (l.g, l.partner)
-        )
-
     def give(self, c, j):
         l = self.lay
-        return remote(self.deal.at[c, j], self.put(c, l.r), self.sg.at[c, j], self.rg.at[c, l.r], (l.g, l.base + j))
-
-    def given(self, c, rr):
-        l = self.lay
-        return remote(self.deal.at[c, l.slot], self.put(c, rr), self.sg.at[c, l.slot], self.rg.at[c, rr], (l.g, l.first + rr))
-
-    def others(self, stage):
-        l = self.lay
-        for rr in range(l.relays):
-            pl.when(l.first + rr != l.me)(functools.partial(stage, rr))
+        return remote(self.deal.at[c, j], self.put(c, l.r, 1), self.s_give, self.r_give.at[c], (l.g, l.base + j))
 
     def lines(self, stage):
         l = self.lay
         for line in range(l.pairs):
             pl.when(jnp.logical_not(l.is_relay) & (line != l.line))(functools.partial(stage, line))
 
-    def near(self, stage):
+    def start_far(self, c):
+        def stage(line):
+            @pl.when(c >= self.early)
+            def _():
+                self.sideways(c, line).start()
+
+            @pl.when(c < self.early)
+            def _():
+                for q in range(self.lay.group):
+                    self.direct(c, line * self.lay.group + q, self.s_early).start()
+
+        self.lines(stage)
+
+    def start_near(self, c):
         l = self.lay
         for rr in range(l.relays):
-            pl.when(jnp.where(l.is_relay, rr != l.r, rr // l.group == l.line))(functools.partial(stage, rr))
-
-    def start_far(self, c):
-        self.lines(lambda line: self.sideways(c, line).start())
-
-    def start_near(self, c):
-        self.near(lambda rr: self.direct(c, rr).start())
+            near = jnp.where(l.is_relay, rr != l.r, rr // l.group == l.line)
+            pl.when(near)(lambda rr=rr: self.direct(c, rr, self.s_direct).start())
 
     def forward(self, c):
         l = self.lay
 
         def stage(line):
-            self.sideways_in(c, line).wait_recv()
             for q in range(l.group):
                 self.onward(c, line, q).start()
 
-        self.lines(stage)
+        if l.pairs > 1:
+            @pl.when(jnp.logical_not(l.is_relay) & (c >= self.early))
+            def _():
+                self.several(self.side.at[c, pl.ds(0, l.pairs - 1)], self.s_side, self.r_side.at[c]).wait_recv()
+                self.lines(stage)
 
     def collect(self, c):
         l = self.lay
@@ -247,8 +241,7 @@
         @pl.when(l.is_relay)
         def _():
             self.pool[c, l.slot] = self.load(c, l.r)
-            for k in range(1, l.half):
-                self.direct_in(c, lax.rem(l.slot + k, l.half)).wait_recv()
+            self.several(self.pool.at[c, pl.ds(0, l.half - 1)], self.s_direct, self.r_direct.at[c]).wait_recv()
             self.over[c] = select(self.cross, self.pool[c, : l.half])
             self.across(c).start()
 
@@ -264,27 +257,38 @@
             self.store(c, l.r, self.deal[c, l.slot])
 
     def arrive(self, c):
-        self.others(lambda rr: self.given(c, rr).wait_recv())
-
-    def drain(self, c):
-        l = self.lay
-        self.near(lambda rr: self.direct(c, rr).wait_send())
-
-        def stage(line):
-            self.sideways(c, line).wait_send()
-            for q in range(l.group):
-                self.onward(c, line, q).wait_send()
-
-        self.lines(stage)
+        l = self.lay
 
         @pl.when(l.is_relay)
         def _():
-            self.across(c).wait_send()
-            for k in range(1, l.half):
-                self.give(c, lax.rem(l.slot + k, l.half)).wait_send()
-
-
-def fused_kernel(d, n, crossing, lags, old, new, routed_hbm, ids, probe, gain, gate_hbm, up_hbm, down_hbm, out, totals,
+            self.several(self.put(c, 0, l.relays - 1), self.s_give, self.r_give.at[c]).wait_recv()
+
+        @pl.when(jnp.logical_not(l.is_relay))
+        def _():
+            self.several(self.put(c, 0, l.relays), self.s_give, self.r_give.at[c]).wait_recv()
+
+    def drain(self):
+        l = self.lay
+
+        @pl.when(l.is_relay)
+        def _():
+            self.several(self.pool.at[:, pl.ds(0, l.relays - 1)], self.s_direct, self.r_direct.at[0]).wait_send()
+            self.several(self.over, self.s_across, self.r_across.at[0]).wait_send()
+            self.several(self.deal.at[:, pl.ds(0, l.half - 1)], self.s_give, self.r_give.at[0]).wait_send()
+
+        @pl.when(jnp.logical_not(l.is_relay))
+        def _():
+            self.several(self.pool.at[:, pl.ds(0, l.group)], self.s_direct, self.r_direct.at[0]).wait_send()
+            if l.pairs > 1:
+                sent = self.side.at[pl.ds(self.early, l.count - self.early), pl.ds(0, l.pairs - 1)]
+                if self.early:
+                    first = self.pool.at[pl.ds(0, self.early), pl.ds(0, l.relays - l.group)]
+                    self.several(first, self.s_early, self.r_side.at[0]).wait_send()
+                self.several(sent, self.s_side, self.r_side.at[0]).wait_send()
+                self.several(sent, self.s_onward, self.r_side.at[0]).wait_send()
+
+
+def fused_kernel(d, n, crossing, old, new, routed_hbm, ids, probe, gain, gate_hbm, up_hbm, down_hbm, out, totals,
                  wg, wu, wd, routed, normed, x, gate_sum, up_sum, hidden, partial, arrived, summed,
                  stats, st_in, st_mid, st_dp, source, holder, order, crossed, pick, cross, pick2, cross2, sl, sw, sd,
                  sy, ry, ss, rs, ssy, rsy, sz, rz, *rest):
@@ -294,73 +298,79 @@
     count, wide, w = lay.count, lay.wide, lay.w
     chunk, piece = lay.chunk, lay.piece
     tall = d * rows
-    down_step = wd.shape[0] // sd.shape[0]
-
-    greet(g, me, d, n)
+    down_parts = 8
+    down_step = wd.shape[0] // down_parts
+
     load_routed = pltpu.make_async_copy(routed_hbm, routed, sl)
     load_routed.start()
+    greet(g, me, d, n)
     weights, downs = [], []
     for c in range(count):
         part = pl.ds(c * wide, wide)
-        weights.append(pltpu.make_async_copy(gate_hbm.at[part, :], wg.at[part, :], sw.at[0, c]))
-        weights.append(pltpu.make_async_copy(up_hbm.at[part, :], wu.at[part, :], sw.at[1, c]))
-    for p in range(sd.shape[0]):
+        weights.append(pltpu.make_async_copy(gate_hbm.at[part, :], wg.at[part, :], sw.at[c]))
+        weights.append(pltpu.make_async_copy(up_hbm.at[part, :], wu.at[part, :], sw.at[c]))
+    for p in range(down_parts):
         part = pl.ds(p * down_step, down_step)
-        downs.append(pltpu.make_async_copy(down_hbm.at[part, :], wd.at[part, :], sd.at[p]))
+        downs.append(pltpu.make_async_copy(down_hbm.at[part, :], wd.at[part, :], sd))
+    load_routed.wait()
+    for load in weights + downs:
+        load.start()
+    mean_square = prepare(routed, probe, gain, normed)
+    meet(d, n)
+
+    def put_x(c, rr, value):
+        x[g, :, piece(c, rr)] = value
+
+    def put_out(c, rr, value):
+        out[:, piece(c, rr)] = value
+
+    there = Route(
+        lay, crossing, min(EARLY[0], count - 1),
+        lambda c, rr, size: normed.at[:, piece(c, rr, size)], lambda c, rr, size: x.at[g, :, piece(c, rr, size)],
+        lambda c, rr: normed[:, piece(c, rr)], put_x, pick, cross, rest[0:4], rest[8:18],
+    )
+    summed_piece = lambda rr, size: pl.ds(pl.multiple_of(rr * w, w), size * w)
+    home = Route(
+        lay, crossing, min(EARLY[1], count - 1),
+        lambda c, rr, size: summed.at[c, :, summed_piece(rr, size)], lambda c, rr, size: out.at[:, piece(c, rr, size)],
+        lambda c, rr: summed[c, :, summed_piece(rr, 1)], put_out, pick2, cross2, rest[4:8], rest[18:28],
+    )
+
+    def peers(ref, send, recv):
+        return remote(ref, ref, send, recv, (lax.rem(g + 1, d), me))
+
+    def along(c, q):
+        here = x.at[g, :, chunk(c)]
+        return remote(here, here, sy, ry.at[c], (lax.rem(g + q, d), me))
+
+    def stat(k):
+        return remote(stats, st_in.at[me], ss, rs, (g, lax.rem(me + k, n)))
+
+    def stat_all():
+        part = st_in.at[pl.ds(0, n - 1)]
+        return remote(part, part, ss, rs, (g, lay.partner))
+
+    def stat_dp(q):
+        return remote(st_mid, st_dp.at[g], ssy, rsy, (lax.rem(g + q, d), me))
+
+    ahead = min(AHEAD, count)
+    pl.loop(0, count)(there.start_far)
+    pl.loop(0, ahead)(there.start_near)
+    pl.when(lay.is_relay)(lambda: pl.loop(ahead, count)(there.start_near))
+
+    @pl.when(jnp.logical_not(lay.is_relay))
+    def _():
+        @pl.loop(0, count)
+        def _(c):
+            there.forward(c)
+            pl.when(c + ahead < count)(lambda: there.start_near(c + ahead))
+
     inverse(old, new, source, n)
     inverse(new, old, holder, n)
     for places, picks, crosses in ((source, pick, cross), (holder, pick2, cross2)):
         plan(places, lay.h, lay.half, crossing, order, crossed)
         selection(picks, order, rows)
         selection(crosses, crossed, rows)
-    load_routed.wait()
-    for load in weights + downs:
-        load.start()
-    mean_square = prepare(routed, probe, gain, normed)
-    meet(d, n)
-
-    def put_x(c, rr, value):
-        x[g, :, piece(c, rr)] = value
-
-    def put_out(c, rr, value):
-        out[:, piece(c, rr)] = value
-
-    there = Route(
-        lay, crossing,
-        lambda c, rr, size: normed.at[:, piece(c, rr, size)], lambda c, rr: x.at[g, :, piece(c, rr)],
-        lambda c, rr: normed[:, piece(c, rr)], put_x, pick, cross, rest[0:4], rest[8:17],
-    )
-    summed_piece = lambda rr, size: pl.ds(pl.multiple_of(rr * w, w), size * w)
-    home = Route(
-        lay, crossing,
-        lambda c, rr, size: summed.at[c, :, summed_piece(rr, size)], lambda c, rr: out.at[:, piece(c, rr)],
-        lambda c, rr: summed[c, :, summed_piece(rr, 1)], put_out, pick2, cross2, rest[4:8], rest[17:26],
-    )
-
-    def along(c, q):
-        here = x.at[g, :, chunk(c)]
-        return remote(here, here, sy.at[c, q], ry.at[c, g], (lax.rem(g + q, d), me))
-
-    def along_in(c, q):
-        f = lax.rem(g + d - q, d)
-        other = x.at[f, :, chunk(c)]
-        return remote(other, other, sy.at[c, q], ry.at[c, f], (f, me))
-
-    def stat(k):
-        return remote(stats, st_in.at[me], ss.at[k], rs.at[me], (g, lax.rem(me + k, n)))
-
-    def stat_in(k):
-        s = lax.rem(me + n - k, n)
-        return remote(stats, st_in.at[s], ss.at[k], rs.at[s], (g, s))
-
-    def stat_dp(q):
-        return remote(st_mid, st_dp.at[g], ssy.at[q], rsy.at[g], (lax.rem(g + q, d), me))
-
-    ahead = min(2, count)
-    pl.loop(0, count)(there.start_far)
-    pl.loop(0, ahead)(there.start_near)
-    pl.when(lay.is_relay)(lambda: pl.loop(ahead, count)(there.start_near))
-
     statistics(ids, mean_square, stats)
     for k in range(1, n):
         stat(k).start()
@@ -368,39 +378,29 @@
     gate_sum[...] = jnp.zeros_like(gate_sum)
     up_sum[...] = jnp.zeros_like(up_sum)
 
-    def forward(c):
-        there.forward(c)
-        pl.when(jnp.logical_not(lay.is_relay) & (c + ahead < count))(lambda: there.start_near(c + ahead))
-
     def take(c):
         there.arrive(c)
         for q in range(1, d):
             along(c, q).start()
 
     def absorb(c):
-        for q in range(1, d):
-            along_in(c, q).wait_recv()
+        if d > 1:
+            peers(x.at[pl.ds(0, d - 1), :, chunk(c)], sy, ry.at[c]).wait_recv()
         part = x[:, :, chunk(c)].astype(jnp.float32).reshape(tall, wide).astype(jnp.bfloat16)
-        for k, (hbm, ref, total) in enumerate(((gate_hbm, wg, gate_sum), (up_hbm, wu, up_sum))):
-            pltpu.make_async_copy(hbm.at[chunk(c), :], ref.at[chunk(c), :], sw.at[k, c]).wait()
+        both = pl.ds(0, 2 * wide)
+        pltpu.make_async_copy(gate_hbm.at[both, :], wg.at[both, :], sw.at[c]).wait()
+        for ref, total in ((wg, gate_sum), (wu, up_sum)):
             total[...] += jnp.dot(part, ref[chunk(c), :], preferred_element_type=jnp.float32)
 
-    pipeline(count, [
-        (forward, 0), (there.collect, lags[0]), (there.hand, lags[1]), (take, lags[2]), (absorb, lags[3]),
-    ])
+    lags = LAGS[count]
+    pipeline(count, [(there.collect, 0), (there.hand, lags[0]), (take, lags[1]), (absorb, lags[2])])
 
     gate = gate_sum[...]
     hidden[...] = (gate / (1.0 + jnp.exp(-gate)) * up_sum[...]).astype(jnp.bfloat16)
-    for load in downs:
-        load.wait()
+    pltpu.make_async_copy(down_hbm, wd, sd).wait()
 
     def home_copy(c, q):
-        t = lax.rem(g + q, d)
-        return remote(partial.at[c, t], arrived.at[c, g], sz.at[c, q], rz.at[c, g], (t, me))
-
-    def home_in(c, q):
-        f = lax.rem(g + d - q, d)
-        return remote(partial.at[c, f], arrived.at[c, f], sz.at[c, q], rz.at[c, f], (f, me))
+        return remote(partial.at[c, lax.rem(g + q, d)], arrived.at[c, q - 1], sz, rz.at[c], (lax.rem(g + q, d), me))
 
     def make(c):
         value = jnp.dot(hidden[...], wd[:, chunk(c)], preferred_element_type=jnp.float32)
@@ -409,17 +409,16 @@
             home_copy(c, q).start()
 
     def add(c):
+        total = partial[c, g].astype(jnp.float32)
+        if d > 1:
+            peers(arrived.at[c], sz, rz.at[c]).wait_recv()
         for q in range(1, d):
-            home_in(c, q).wait_recv()
-        total = partial[c, g].astype(jnp.float32)
-        for q in range(1, d):
-            total = total + arrived[c, lax.rem(g + q, d)].astype(jnp.float32)
+            total = total + arrived[c, q - 1].astype(jnp.float32)
         summed[c] = total.astype(jnp.bfloat16)
         home.start_far(c)
         home.start_near(c)
 
-    for k in range(1, n):
-        stat_in(k).wait_recv()
+    stat_all().wait_recv()
     mid = st_in[0]
     for s in range(1, n):
         mid = mid + st_in[s]
@@ -429,30 +428,21 @@
         stat_dp(q).start()
 
     pipeline(count, [
-        (make, 0), (add, lags[4]), (home.forward, lags[5]), (home.collect, lags[6]), (home.hand, lags[7]),
+        (make, 0), (add, lags[3]), (home.forward, lags[4]), (home.collect, lags[5]), (home.hand, lags[6]),
     ])
 
-    for q in range(1, d):
-        f = lax.rem(g + d - q, d)
-        remote(st_mid, st_dp.at[f], ssy.at[q], rsy.at[f], (f, me)).wait_recv()
+    stat_all().wait_send()
+    if d > 1:
+        peers(st_dp.at[pl.ds(0, d - 1)], ssy, rsy).wait()
+        peers(x.at[pl.ds(0, d - 1)], sy, ry.at[0]).wait_send()
+        peers(arrived, sz, rz.at[0]).wait_send()
     total = st_dp[0]
     for f in range(1, d):
         total = total + st_dp[f]
     totals[...] = total
 
-    for k in range(1, n):
-        stat(k).wait_send()
-    for q in range(1, d):
-        stat_dp(q).wait_send()
-
-    @pl.loop(0, count)
-    def _(c):
-        there.drain(c)
-        home.drain(c)
-        for q in range(1, d):
-            along(c, q).wait_send()
-            home_copy(c, q).wait_send()
-
+    there.drain()
+    home.drain()
     pl.loop(0, count)(home.arrive)
 
 
@@ -472,12 +462,9 @@
         block(count, pairs, rows, group * w), block(count, half + crossing, rows, w),
         block(count, crossing, rows, w), block(count, half, rows, w),
     ]
-    sems = [
-        dma((count, relays)), dma((count, half)), dma((count, pairs)), dma((count, pairs)), dma((count, pairs, group)),
-        dma((count,)), dma((count,)), dma((count, half)), dma((count, relays)),
-    ]
+    sems = [dma, dma, dma, dma, dma, dma, dma((count,)), dma((count,)), dma((count,)), dma((count,))]
     return pl.pallas_call(
-        functools.partial(fused_kernel, d, n, crossing, LAGS),
+        functools.partial(fused_kernel, d, n, crossing),
         out_shape=(
             jax.ShapeDtypeStruct((rows, width), jnp.bfloat16),
             jax.ShapeDtypeStruct((2, experts), jnp.float32),
@@ -488,16 +475,15 @@
             block(width, units), block(width, units), block(units, width),
             block(tokens, width), block(rows, width), block(d, rows, width),
             wide(d * rows, units), wide(d * rows, units), block(d * rows, units),
-            block(count, d, rows, full), block(count, d, rows, full), block(count, rows, full),
+            block(count, d, rows, full), block(count, max(1, d - 1), rows, full), block(count, rows, full),
             wide(2, experts), wide(n, 2, experts), wide(2, experts), wide(d, 2, experts),
             numbers(n), numbers(n), numbers(half), numbers(crossing), *matrices, *matrices,
-            dma, dma((2, count)), dma((8,)),
-            dma((count, d)), dma((count, d)), dma((n,)), dma((n,)), dma((d,)), dma((d,)),
-            dma((count, d)), dma((count, d)),
+            dma, dma((count,)), dma,
+            dma, dma((count,)), dma, dma, dma, dma, dma, dma((count,)),
             *bufs, *bufs, *sems, *sems,
         ],
         compiler_params=pltpu.CompilerParams(
-            collective_id=collective, has_side_effects=True, vmem_limit_bytes=62 << 20
+            collective_id=collective, has_side_effects=True, vmem_limit_bytes=125 << 19
         ),
     )(old, new, routed, ids, probe, gain, gate, up, down)
 

time: 79.1 us -> 73.6 us (0.930)
  Pallas kernels: 73.1 us -> 67.8 us
    pallas_call x1, Pallas kernels: 73.1 us -> 67.8 us  [fused(): pl.pallas_call(functools.partial(fused_kernel, d, n, crossing), out_shape...]
where the time goes in v2:
time: 73.6 us; the launch traced here: 73.3 us
  Pallas kernels  67.8 us (92%)
  between operations  1.96 us (3%)
  other arithmetic  1.91 us (3%)
  local copies, waits for them, and re-layouts  1.62 us (2%)
    pallas_call x1, Pallas kernels, fused(): pl.pallas_call(functools.partial(fused_kernel, d, n, crossing), out_shape...  67.8 us

profile of v2, /device:TPU:0, one launch (start us, length us, event | category | flops | bytes accessed | tf_op | source)
XLA Modules:
  0.0 73.3 jit_solution(3063893690198612504)
XLA Ops:
  0.6 1.4 %convert_reduce_fusion = s32[]{:T(128)} fusion(s32[16]{0:T(128)} %param.19, s32[16]{0:T(128)} %param.18, pred[16]{0:T(512)(128)(4,1)S(1)} %get-tuple-element.90, pred[16]{0:T(512)(128)(4,1)S(1)} %get-tuple-element.91), kind=kLoop, calls=%fused_computation | loop fusion | flops 1279 | bytes 164 | tf_op jit(solution)/shard_map/reduce_sum | solution.py:509
  3.3 0.7 reshape.28
  4.1 67.8 %conditional.1 = ((bf16[40,7168]{1,0:T(8,128)(2,1)S(1)}, f32[2,128]{1,0:T(2,128)S(1)})) conditional(s32[]{:T(128)} %clamp.3, (s32[16]{0:T(128)}, s32[16]{0:T(128)}, bf16[128,7168]{1,0:T(8,128)(2,1)}, s32[8,128]{1,0:T(8,128)}, s32[1,40]{1,0:T(1,128)}, /*index=5*/bf16[1,7168]{1,0:T(2,128)(2,1)S(1)}, bf16[7168,1024]{1,0:T(8,128)(2,1)}, ...), branch_computations={%region_1.0_spmd, %region_2.0_spmd, %region_3.0_spmd} | conditional | bytes 8 | solution.py:512
  4.1 67.8 %branch_1_fun.1 = (bf16[40,7168]{1,0:T(8,128)(2,1)S(1)}, f32[2,128]{1,0:T(2,128)S(1)}) custom-call(s32[16]{0:T(128)} %get-tuple-element.63.old, s32[16]{0:T(128)} %get-tuple-element.64.new, bf16[128,7168]{1,0:T(8,128)(2,1)} %get-tuple-element.65.routed_hbm, s32[8,128]{1,0:T(8,128)} %get-tuple-element.66.ids, s32[1,40]{1,0:T(1,128)} %get-tuple-element.67.probe, ...), custom_call_target="tpu_custom_call" | custom-call | tf_op jit(solution)/shard_map/cond/branch_1_fun/pallas_call | solution.py:466
  71.9 0.1 constant_dynamic-slice_fusion
  71.9 0.5 fusion
  72.5 0.8 %copy.19 = bf16[40,7168]{1,0:T(8,128)(2,1)} copy(bf16[40,7168]{1,0:T(8,128)(2,1)S(1)} %get-tuple-element.103) | data formatting | bytes 1146880
  (1 shorter events, 0.0 us)

commit v3 on v2

--- a/solution.py
+++ b/solution.py
@@ -16,9 +16,10 @@
 epsilon = 1e-06
 PAIR = 2
 AHEAD = 4
-EARLY = (3, 3)
+FIRST = (4, 0)
+SECOND = (7, 3)
 MOST = 14
-LAGS = {7: (2, 4, 6, 1, 2, 4, 6), 14: (4, 8, 12, 3, 5, 7, 10)}
+LAGS = {7: (2, 4, 6, 2, 3, 4, 6), 14: (4, 7, 11, 4, 6, 8, 11)}
 
 
 def chunking(width, relays):
@@ -26,6 +27,11 @@
     assert units * relays * LANES == width
     count = max(c for c in range(1, MOST + 1) if units % c == 0)
     return count, units // count * LANES
+
+
+def direct_chunks(count, wanted):
+    early = min(wanted[0], count // 2)
+    return early, min(wanted[1], count // 4)
 
 
 def remote(src, dst, send, recv, device):
@@ -64,7 +70,7 @@
     for c in range(width // step):
         cols = slice(c * step, (c + 1) * step)
         rows = jnp.dot(pick, routed[:, cols], preferred_element_type=jnp.float32)
-        normed[:, cols] = (rows * scale * gain[:, cols].astype(jnp.float32)).astype(jnp.bfloat16)
+        normed[:, cols] = (rows * scale * gain[cols].astype(jnp.float32)[None, :]).astype(jnp.bfloat16)
     return mean_square
 
 
@@ -165,7 +171,8 @@
         self.side, self.pool, self.over, self.deal = bufs
         self.s_direct, self.s_early, self.s_side, self.s_onward, self.s_across, self.s_give = sems[:6]
         self.r_direct, self.r_side, self.r_across, self.r_give = sems[6:]
-        self.early = early
+        self.early, self.late = early
+        self.few = self.early + self.late
 
     def several(self, ref, send, recv):
         return remote(ref, ref, send, recv, (self.lay.g, self.lay.partner))
@@ -203,13 +210,16 @@
         for line in range(l.pairs):
             pl.when(jnp.logical_not(l.is_relay) & (line != l.line))(functools.partial(stage, line))
 
+    def through(self, c):
+        return (c >= self.early) & (c < self.lay.count - self.late)
+
     def start_far(self, c):
         def stage(line):
-            @pl.when(c >= self.early)
+            @pl.when(self.through(c))
             def _():
                 self.sideways(c, line).start()
 
-            @pl.when(c < self.early)
+            @pl.when(jnp.logical_not(self.through(c)))
             def _():
                 for q in range(self.lay.group):
                     self.direct(c, line * self.lay.group + q, self.s_early).start()
@@ -230,7 +240,7 @@
                 self.onward(c, line, q).start()
 
         if l.pairs > 1:
-            @pl.when(jnp.logical_not(l.is_relay) & (c >= self.early))
+            @pl.when(jnp.logical_not(l.is_relay) & self.through(c))
             def _():
                 self.several(self.side.at[c, pl.ds(0, l.pairs - 1)], self.s_side, self.r_side.at[c]).wait_recv()
                 self.lines(stage)
@@ -280,9 +290,9 @@
         def _():
             self.several(self.pool.at[:, pl.ds(0, l.group)], self.s_direct, self.r_direct.at[0]).wait_send()
             if l.pairs > 1:
-                sent = self.side.at[pl.ds(self.early, l.count - self.early), pl.ds(0, l.pairs - 1)]
-                if self.early:
-                    first = self.pool.at[pl.ds(0, self.early), pl.ds(0, l.relays - l.group)]
+                sent = self.side.at[pl.ds(0, l.count - self.few), pl.ds(0, l.pairs - 1)]
+                if self.few:
+                    first = self.pool.at[pl.ds(0, self.few), pl.ds(0, l.relays - l.group)]
                     self.several(first, self.s_early, self.r_side.at[0]).wait_send()
                 self.several(sent, self.s_side, self.r_side.at[0]).wait_send()
                 self.several(sent, self.s_onward, self.r_side.at[0]).wait_send()
@@ -325,13 +335,13 @@
         out[:, piece(c, rr)] = value
 
     there = Route(
-        lay, crossing, min(EARLY[0], count - 1),
+        lay, crossing, direct_chunks(count, FIRST),
         lambda c, rr, size: normed.at[:, piece(c, rr, size)], lambda c, rr, size: x.at[g, :, piece(c, rr, size)],
         lambda c, rr: normed[:, piece(c, rr)], put_x, pick, cross, rest[0:4], rest[8:18],
     )
     summed_piece = lambda rr, size: pl.ds(pl.multiple_of(rr * w, w), size * w)
     home = Route(
-        lay, crossing, min(EARLY[1], count - 1),
+        lay, crossing, direct_chunks(count, SECOND),
         lambda c, rr, size: summed.at[c, :, summed_piece(rr, size)], lambda c, rr, size: out.at[:, piece(c, rr, size)],
         lambda c, rr: summed[c, :, summed_piece(rr, 1)], put_out, pick2, cross2, rest[4:8], rest[18:28],
     )
@@ -392,7 +402,7 @@
         for ref, total in ((wg, gate_sum), (wu, up_sum)):
             total[...] += jnp.dot(part, ref[chunk(c), :], preferred_element_type=jnp.float32)
 
-    lags = LAGS[count]
+    lags = LAGS[count] if count in LAGS else LAGS[7]
     pipeline(count, [(there.collect, 0), (there.hand, lags[0]), (take, lags[1]), (absorb, lags[2])])
 
     gate = gate_sum[...]
@@ -511,7 +521,7 @@
     kernels = [functools.partial(fused, widths[i], i, d, n, experts) for i in range(3)]
     probe_out, totals = lax.switch(
         branch, kernels,
-        old_place, new_place, routed, expert_ids.T, probe_ids.reshape(1, -1), norm_gain.reshape(1, -1),
+        old_place, new_place, routed, expert_ids.T, probe_ids.reshape(1, -1), norm_gain,
         gate_weight[0], up_weight[0], down_weight[0],
     )
     owned = lax.dynamic_slice_in_dim(totals, lax.axis_index("expert") * EXP_DEV, EXP_DEV, 1)

time: 73.6 us -> 68.7 us (0.933)
  Pallas kernels: 67.8 us -> 63.7 us
  local copies, waits for them, and re-layouts: 1.62 us -> 0.88 us
    pallas_call x1, Pallas kernels: 67.8 us -> 63.7 us  [fused(): pl.pallas_call(functools.partial(fused_kernel, d, n, crossing), out_shape...]
where the time goes in v3:
time: 68.7 us; the launch traced here: 68.5 us
  Pallas kernels  63.7 us (93%)
  between operations  1.95 us (3%)
  other arithmetic  1.91 us (3%)
  local copies, waits for them, and re-layouts  0.88 us (1%)
    pallas_call x1, Pallas kernels, fused(): pl.pallas_call(functools.partial(fused_kernel, d, n, crossing), out_shape...  63.7 us
    reduce_sum x1, other arithmetic, on_device(): jnp.sum(((old_place[:, None] == new_place[None, :]) & apart).astype(jnp.i...  1.38 us

profile of v3, /device:TPU:0, one launch (start us, length us, event | category | flops | bytes accessed | tf_op | source)
XLA Modules:
  0.0 68.5 jit_solution(893023342026640219)
XLA Ops:
  0.6 1.4 %convert_reduce_fusion = s32[]{:T(128)} fusion(s32[16]{0:T(128)} %param.19, s32[16]{0:T(128)} %param.18, pred[16]{0:T(512)(128)(4,1)S(1)} %get-tuple-element.90, pred[16]{0:T(512)(128)(4,1)S(1)} %get-tuple-element.91), kind=kLoop, calls=%fused_computation | loop fusion | flops 1279 | bytes 164 | tf_op jit(solution)/shard_map/reduce_sum | solution.py:519
  3.3 63.7 %conditional.1 = ((bf16[40,7168]{1,0:T(8,128)(2,1)S(1)}, f32[2,128]{1,0:T(2,128)S(1)})) conditional(s32[]{:T(128)} %clamp.3, (s32[16]{0:T(128)}, s32[16]{0:T(128)}, bf16[128,7168]{1,0:T(8,128)(2,1)}, s32[8,128]{1,0:T(8,128)}, s32[1,40]{1,0:T(1,128)}, /*index=5*/bf16[7168]{0:T(1024)(128)(2,1)}, bf16[7168,1024]{1,0:T(8,128)(2,1)}, ...), branch_computations={%region_1.0_spmd, %region_2.0_spmd, %region_3.0_spmd} | conditional | bytes 8 | solution.py:522
  3.3 63.7 %branch_0_fun.1 = (bf16[40,7168]{1,0:T(8,128)(2,1)S(1)}, f32[2,128]{1,0:T(2,128)S(1)}) custom-call(s32[16]{0:T(128)} %get-tuple-element.54.old, s32[16]{0:T(128)} %get-tuple-element.55.new, bf16[128,7168]{1,0:T(8,128)(2,1)} %get-tuple-element.56.routed_hbm, s32[8,128]{1,0:T(8,128)} %get-tuple-element.57.ids, s32[1,40]{1,0:T(1,128)} %get-tuple-element.58.probe, ...), custom_call_target="tpu_custom_call" | custom-call | tf_op jit(solution)/shard_map/cond/branch_0_fun/pallas_call | solution.py:476
  67.1 0.1 constant_dynamic-slice_fusion
  67.1 0.5 fusion
  67.7 0.8 %copy.19 = bf16[40,7168]{1,0:T(8,128)(2,1)} copy(bf16[40,7168]{1,0:T(8,128)(2,1)S(1)} %get-tuple-element.103) | data formatting | bytes 1146880
  (1 shorter events, 0.0 us)
